TPU v7x, 256 devices: a whole 4x4x8 slice. The times are simulated.
256 devices in a mesh: section: 16 (over z_lo, x), tensor: 16 (over z_hi, y, core).
Axes of the slice: x: 4, y: 4, z: 8 (z_hi: 2, z_lo: 4; z = z_hi * 4 + z_lo), core: 2. Of those that a mesh axis runs over, the one named last changes fastest.
Arguments:
- hidden: bfloat16 [256, 8192], P(('section', 'tensor')), may hold values from -12 to 12
- weight: bfloat16 [131072, 8192], P(('section', 'tensor')), may hold values from -1 to 1
- targets: int32 [256], replicated, may hold values from 0 to 131071
- loss_grad: float32 [256], P(('section', 'tensor')), may hold values from 8 to 64
Outputs:
- token_loss: float32 [256], P(('section', 'tensor'))
- hidden_grad: bfloat16 [256, 8192], P(('section', 'tensor'))
All inputs are finite; a program needn't handle non-finite values.
Results may differ from a plain program's by a relative error of at most 0.0039.
Values may be sent and summed in bfloat16 or wider, within the bound.
A program may use at most 64 MiB of HBM per device.

v0:
```python
import jax
import jax.numpy as jnp
from jax import lax
from jax.sharding import Mesh
from jax.sharding import PartitionSpec as P

TENSOR = ("tensor_0", "tensor_1", "tensor_2")
SECTION = ("section_0", "section_1")
SECTION_TENSOR = ("section_0", "section_1", "tensor_0", "tensor_1", "tensor_2")


def collected_together(array, axis):
    leaves = jax.tree.leaves(array)
    order = sorted(range(len(leaves)), key=lambda k: -leaves[k].size)
    width = (1, *leaves[order[0]].shape)[-1]
    lines = [
        jnp.pad(leaves[k].reshape(-1), (0, -leaves[k].size % width)).reshape(-1, width)
        for k in order
    ]
    both, at, found = (lax.all_gather(jnp.concatenate(lines), axis), 0, {})
    for k, line in zip(order, lines):
        slab = both[:, at : at + len(line)].reshape(len(both), -1)
        found[k] = slab[:, : leaves[k].size].reshape(-1, *leaves[k].shape)
        at += len(line)
    numbers = iter(range(len(leaves)))
    return jax.tree.map(lambda _: found[next(numbers)], array)


def joined_all(array, axes, combine):
    for axis in axes:
        pieces = collected_together(array, axis)
        array = jax.tree.map(lambda part: part[0], pieces)
        for k in range(1, lax.axis_size(axis)):
            array = combine(array, jax.tree.map(lambda part: part[k], pieces))
    return array


def cut_along(array, dim, peers):
    before, after = (array.shape[:dim], array.shape[dim + 1 :])
    return jnp.moveaxis(array.reshape(*before, peers, -1, *after), dim, 0)


def sent_and_summed(array, axis, dim):
    peers = lax.axis_size(axis)
    pieces = lax.all_to_all(cut_along(array, dim, peers), axis, 0, 0, tiled=True)
    return jnp.sum(pieces, axis=0)


def combine_parts(left_part, right_part):
    largest = jnp.maximum(left_part[0], right_part[0])
    summed = left_part[1] * jnp.exp(left_part[0] - largest) + right_part[1] * jnp.exp(
        right_part[0] - largest
    )
    return (largest, summed, left_part[2] + right_part[2])


def shards(hidden, weight, targets, loss_grad):
    tok_dev = hidden.shape[0]
    vocab_dev = weight.shape[0]
    section_block = lax.all_gather(hidden, TENSOR, axis=0, tiled=True)
    logits = lax.dot_general(
        lax.all_gather(section_block, SECTION, axis=0, tiled=True),
        weight,
        (((1,), (1,)), ((), ())),
        preferred_element_type=jnp.float32,
    )
    my_index = lax.axis_index(SECTION_TENSOR)
    offset = my_index * vocab_dev
    columns = offset + lax.broadcasted_iota(jnp.int32, (1, vocab_dev), 1)
    target_mask = columns == targets[:, None]
    local_target = jnp.sum(jnp.where(target_mask, logits, 0.0), axis=1)
    local_max = jnp.max(logits, axis=1)
    local_shift = jnp.exp(logits - local_max[:, None])
    local_total = jnp.sum(local_shift, axis=1)
    row_max, exp_total, target_logit = joined_all(
        (local_max, local_total, local_target), SECTION_TENSOR, combine_parts
    )
    shifted = local_shift * jnp.exp(local_max - row_max)[:, None]
    probs_grad = (shifted / exp_total[:, None] - target_mask.astype(jnp.float32)).astype(
        jnp.bfloat16
    )
    all_loss = row_max + jnp.log(exp_total) - target_logit
    token_loss = lax.dynamic_slice_in_dim(all_loss, my_index * tok_dev, tok_dev)
    section_part = lax.psum_scatter(
        jnp.dot(probs_grad, weight, preferred_element_type=jnp.float32),
        SECTION,
        scatter_dimension=0,
        tiled=True,
    )
    grad_sum = sent_and_summed(section_part, TENSOR, 0)
    hidden_grad = (loss_grad[:, None] * grad_sum).astype(jnp.bfloat16)
    return (token_loss, hidden_grad)


def solution(mesh):
    finer = Mesh(
        mesh.devices.reshape(4, 4, 2, 4, 2),
        ("section_0", "section_1", "tensor_0", "tensor_1", "tensor_2"),
    )
    in_specs = (P(SECTION_TENSOR, None), P(SECTION_TENSOR, None), P(), P(SECTION_TENSOR))
    out_specs = (P(SECTION_TENSOR), P(SECTION_TENSOR, None))
    return jax.shard_map(
        shards, mesh=finer, in_specs=in_specs, out_specs=out_specs, check_vma=False
    )
```

profile of v0, /device:TPU:1, one launch (start us, length us, event | category | flops | bytes accessed | tf_op | source)
XLA Modules:
  0.0 328.5 jit_solution(14433326831558303226)
XLA Ops:
  7.2 0.0 all-gather.13.cloned.1.call-start
  7.2 36.5 %all-gather.5 = bf16[16,1,8192]{2,1,0:T(2,128)(2,1)S(1)} all-gather(bf16[1,1,8192]{2,1,0:T(2,128)(2,1)} %bitcast.281), channel_id=1, replica_groups=mesh['section_0'=4,'section_1'=4,'tensor_0'=2,'tensor_1'=4,'tensor_2'=2]..., dimensions={0}, use_global_device_ids=true | all-gather | bytes 278528 | tf_op jit(solution)/shard_map/all_gather | solution.py:60
  43.7 0.0 copy-start
  43.7 1.0 copy.9
  44.7 0.0 all-gather.13.cloned.1.call-update
  44.7 0.0 reduce-scatter.2.cloned.1.call-start
  44.8 72.8 %all-gather.13.cloned.1.call-done = bf16[256,8192]{1,0:T(8,128)(2,1)} async-done(((bf16[16,8192]{1,0:T(8,128)(2,1)}), bf16[256,8192]{1,0:T(8,128)(2,1)}) %all-gather.13.cloned.1.call-update) | async-done | bytes 4194320 | tf_op jit(solution)/shard_map/all_gather | solution.py:62
  117.5 7.1 %fusion.60 = (f32[256]{0:T(256)S(1)}, f32[256,512]{1,0:T(8,128)S(1)}) fusion(bf16[256,8192]{1,0:T(8,128)(2,1)} %all-gather.13.cloned.1.call-done, bf16[512,8192]{1,0:T(8,128)(2,1)} %param.5), kind=kOutput, calls=%fused_computation.108 | convolution fusion | flops 2147614464 | bytes 13108224 | tf_op jit(solution)/shard_map/dot_general | solution.py:61
  124.6 0.0 copy-done
  124.7 0.3 fusion.3
  124.9 10.3 %all-gather.6 = f32[4,3,256]{2,1,0:T(4,128)S(1)} all-gather(f32[1,3,256]{2,1,0:T(4,128)S(1)} %maximum_bitcast_fusion), channel_id=2, replica_groups=mesh['section_0'=4,'section_1'=4,'tensor_0'=2,'tensor_1'=4,'tensor_2'=2]..., dimensions={0}, use_global_device_ids=true | all-gather | bytes 15360 | tf_op jit(solution)/shard_map/all_gather | solution.py:20
  135.3 9.1 %all-gather.7 = f32[4,3,256]{2,1,0:T(4,128)S(1)} all-gather(f32[1,3,256]{2,1,0:T(4,128)S(1)} %maximum_bitcast_fusion.1), channel_id=3, replica_groups=mesh['section_0'=4,'section_1'=4,'tensor_0'=2,'tensor_1'=4,'tensor_2'=2]..., dimensions={0}, use_global_device_ids=true | all-gather | bytes 15360 | tf_op jit(solution)/shard_map/all_gather | solution.py:20
  144.5 7.1 %all-gather.8 = f32[2,3,256]{2,1,0:T(4,128)S(1)} all-gather(f32[1,3,256]{2,1,0:T(4,128)S(1)} %maximum_bitcast_fusion.2), channel_id=4, replica_groups=mesh['section_0'=4,'section_1'=4,'tensor_0'=2,'tensor_1'=4,'tensor_2'=2]..., dimensions={0}, use_global_device_ids=true | all-gather | bytes 9216 | tf_op jit(solution)/shard_map/all_gather | solution.py:20
  151.7 9.5 %all-gather.9 = f32[4,3,256]{2,1,0:T(4,128)S(1)} all-gather(f32[1,3,256]{2,1,0:T(4,128)S(1)} %maximum_bitcast_fusion.3), channel_id=5, replica_groups=mesh['section_0'=4,'section_1'=4,'tensor_0'=2,'tensor_1'=4,'tensor_2'=2]..., dimensions={0}, use_global_device_ids=true | all-gather | bytes 15360 | tf_op jit(solution)/shard_map/all_gather | solution.py:20
  161.2 20.6 %all-gather.10 = f32[2,3,256]{2,1,0:T(4,128)S(1)} all-gather(f32[1,3,256]{2,1,0:T(4,128)S(1)} %maximum_bitcast_fusion.4), channel_id=6, replica_groups=mesh['section_0'=4,'section_1'=4,'tensor_0'=2,'tensor_1'=4,'tensor_2'=2]..., dimensions={0}, use_global_device_ids=true | all-gather | bytes 9216 | tf_op jit(solution)/shard_map/all_gather | solution.py:20
  181.9 9.1 %fusion.4 = f32[256,8192]{1,0:T(8,128)} fusion(bf16[512,8192]{1,0:T(8,128)(2,1)} %param.5, f32[256,512]{1,0:T(8,128)S(1)} %get-tuple-element.22, f32[256]{0:T(256)S(1)} %get-tuple-element.7, f32[256]{0:T(256)S(1)} %get-tuple-element.4, s32[512]{0:T(512)S(1)} %iota_add_fusion, f32[256]{0:T(256)S(1)} %get-tuple-element.21, s32[256]{0:T(256)S(1)} %copy-done), kind=kOutput, calls=%fused_computation.7 | convolution fusion | flops 2148401152 | bytes 17307648 | tf_op jit(solution)/shard_map/dot_general | solution.py:85
  190.9 0.0 reduce-scatter.2.cloned.1.call-update
  191.0 97.7 %reduce-scatter.2.cloned.1.call-done = f32[16,8192]{1,0:T(8,128)} async-done(((f32[256,8192]{1,0:T(8,128)}), f32[16,8192]{1,0:T(8,128)}) %reduce-scatter.2.cloned.1.call-update) | async-done | bytes 524304 | tf_op jit(solution)/shard_map/reduce_scatter | solution.py:84
  288.7 2.4 copy.6
  291.1 16.0 %all-to-all-start = ((f32[16,1,8192]{2,1,0:T(1,128)}), f32[16,1,8192]{2,1,0:T(1,128)S(1)}, u32[]{:S(2)}, u32[]{:S(2)}) async-start(f32[16,1,8192]{2,1,0:T(1,128)} %copy.6), calls=%async_computation.1 | async-start | bytes 1048576 | tf_op jit(solution)/shard_map/all_to_all | solution.py:45
  307.7 0.6 dynamic_slice.3
  308.3 12.3 %all-to-all-done = f32[16,1,8192]{2,1,0:T(1,128)S(1)} async-done(((f32[16,1,8192]{2,1,0:T(1,128)}), f32[16,1,8192]{2,1,0:T(1,128)S(1)}, u32[]{:S(2)}, u32[]{:S(2)}) %all-to-all-start) | async-done | bytes 524320 | tf_op jit(solution)/shard_map/all_to_all | solution.py:45
  320.6 0.3 reduce_sum.29
  321.0 0.6 convert_element_type.23
  (18 shorter events, 0.2 us)
Async XLA Ops:
  7.2 110.4 %all-gather.13.cloned.1.call-start = ((), (), s32[]{:S(2)}) async-start(), calls=%async_computation.2 | async-start | bytes 4456448 | tf_op jit(solution)/shard_map/all_gather | solution.py:62
  43.7 81.0 %copy-start = (s32[256]{0:T(256)S(1)}, s32[256]{0:T(256)}, u32[]{:S(2)}) copy-start(s32[256]{0:T(256)} %param.6) | copy-start | bytes 3076
  44.7 244.0 %reduce-scatter.2.cloned.1.call-start = ((), (), s32[]{:S(2)}) async-start(), calls=%async_computation.3 | async-start | bytes 8912896 | tf_op jit(solution)/shard_map/reduce_scatter | solution.py:84
  291.1 29.5 %all-to-all-start = ((f32[16,1,8192]{2,1,0:T(1,128)}), f32[16,1,8192]{2,1,0:T(1,128)S(1)}, u32[]{:S(2)}, u32[]{:S(2)}) async-start(f32[16,1,8192]{2,1,0:T(1,128)} %copy.6), calls=%async_computation.1 | async-start | bytes 1048576 | tf_op jit(solution)/shard_map/all_to_all | solution.py:45
Sparse Core Ops, SparseCore 0:
  44.8 72.6 all-gather.12
  191.1 97.5 reduce-scatter.1
where the time goes:
time: 329 us; the launch traced here: 328 us
  waiting for transfers between devices  183 us (56%)
  blocking collectives  93.1 us (28%)
  matrix products  16.2 us (5%)
  starting transfers between devices  16.1 us (5%)
  between operations  14.8 us (4%)
  local copies, waits for them, and re-layouts  4.59 us (1%)
    reduce_scatter x1, waiting for transfers between devices, shards(): lax.psum_scatter(jnp.dot(probs_grad, weight, preferred_element_type=jnp.f...  97.7 us
    all_gather x1, waiting for transfers between devices, shards(): lax.all_gather(section_block, SECTION, axis=0, tiled=True)  72.8 us
    all_gather x5, blocking collectives, collected_together(): both, at, found = (lax.all_gather(jnp.concatenate(lines), axis), 0, {})  56.7 us
    all_gather x1, blocking collectives, shards(): section_block = lax.all_gather(hidden, TENSOR, axis=0, tiled=True)  36.5 us
    all_to_all x1, starting transfers between devices, sent_and_summed(): lax.all_to_all(cut_along(array, dim, peers), axis, 0, 0, tiled=True)  16 us
    all_to_all x1, waiting for transfers between devices, sent_and_summed(): lax.all_to_all(cut_along(array, dim, peers), axis, 0, 0, tiled=True)  12.3 us
    dot_general x1, matrix products, shards(): jnp.dot(probs_grad, weight, preferred_element_type=jnp.float32)  9.08 us
    dot_general x1, matrix products, shards(): lax.dot_general(lax.all_gather(section_block, SECTION, axis=0, tiled=True...  7.1 us
  transfers between devices with their start and end apart: 3, of which 3 were waited for; matrix products, arithmetic and copies ran while one was open for 0% of the time, Pallas kernels for 0%

commit v1 on v0

v1 whole, which is shorter than its diff:
```python
import jax
import jax.numpy as jnp
from jax import lax
from jax.experimental import pallas as pl
from jax.experimental.pallas import tpu as pltpu
from jax.sharding import Mesh
from jax.sharding import PartitionSpec as P

AXES = ("zl", "x", "zh", "y", "c")
F32, BF16 = jnp.float32, jnp.bfloat16
QUARTER = 2048
LANES = 128


class Sems:
    def __init__(self, send, recv):
        self.send, self.recv, self.next = send, recv, 0

    def take(self):
        k = self.next
        self.next += 1
        return self.send.at[k], self.recv.at[k]


def kernel(
    h_ref, w_hbm, tgt_ref, lg_ref, loss_ref, grad_ref,
    wv, row_f, row_b, got, wide, hid, logits, pt, stat, st1, st2, own_sum, give, take,
    ub, vb_opp, vb_all, ua, va_opp, va_all, acc_a, rows_out, rows_b, rows_in,
    w_sem, send_sem, recv_sem,
):
    zl, x, zh, y, c = (lax.axis_index(a) for a in AXES)
    z = zh * 4 + zl
    sems = Sems(send_sem, recv_sem)
    pending = []

    def device(x_, y_, z_, c_):
        return (lax.rem(z_, 4), x_, lax.div(z_, 4), y_, c_)

    def send(src, dst, to):
        s, r = sems.take()
        copy = pltpu.make_async_remote_copy(
            src_ref=src, dst_ref=dst, send_sem=s, recv_sem=r,
            device_id=to, device_id_type=pl.DeviceIdType.MESH,
        )
        copy.start()
        pending.append(copy)
        return copy

    up = {"x": lax.rem(x + 1, 4), "y": lax.rem(y + 1, 4)}
    opp = {"x": lax.rem(x + 2, 4), "y": lax.rem(y + 2, 4)}
    down = {"x": lax.rem(x + 3, 4), "y": lax.rem(y + 3, 4)}
    here = {"x": x, "y": y}

    def to_up(axis):
        return device(up["x"] if axis == "x" else x, up["y"] if axis == "y" else y, z, c)

    def to_down(axis):
        return device(down["x"] if axis == "x" else x, down["y"] if axis == "y" else y, z, c)

    partner = device(x, y, z, 1 - c)
    column = [(dz, dc) for dz in range(8) for dc in range(2) if (dz, dc) != (0, 0)]
    plane = [(dx, dy) for dx in range(4) for dy in range(4) if (dx, dy) != (0, 0)]

    def in_column(dz, dc):
        return lax.rem(z + dz, 8), lax.rem(c + dc, 2)

    def in_plane(dx, dy):
        return lax.rem(x + dx, 4), lax.rem(y + dy, 4)

    w_copies = [
        pltpu.make_async_copy(
            w_hbm.at[:, pl.ds(q * QUARTER, QUARTER)], wv.at[:, pl.ds(q * QUARTER, QUARTER)], w_sem.at[q]
        )
        for q in range(4)
    ]
    for copy in w_copies:
        copy.start()

    barrier = pltpu.get_barrier_semaphore()
    for dz, dc in column:
        z_, c_ = in_column(dz, dc)
        pl.semaphore_signal(barrier, inc=1, device_id=device(x, y, z_, c_), device_id_type=pl.DeviceIdType.MESH)
    for dx, dy in plane:
        x_, y_ = in_plane(dx, dy)
        pl.semaphore_signal(barrier, inc=1, device_id=device(x_, y_, z, c), device_id_type=pl.DeviceIdType.MESH)

    for k in range(64):
        row_f[pl.ds(k, 1), :] = h_ref[:, pl.ds(k * LANES, LANES)].astype(F32)
    row_b[...] = row_f[...].astype(BF16)
    me = z * 2 + c

    pl.semaphore_wait(barrier, len(column) + len(plane))

    arrivals = []
    for dz, dc in column:
        z_, c_ = in_column(dz, dc)
        arrivals.append(
            send(row_b.at[pl.ds(pl.multiple_of(c_ * 32, 32), 32)], got.at[me], device(x, y, z_, c_))
        )
    got[me] = row_b[pl.ds(pl.multiple_of(c * 32, 32), 32), :]
    for copy in arrivals:
        copy.wait_recv()
    wide[...] = got[...].astype(F32)
    for k in range(32):
        hid[2 * c + k // 16, y, x, :, pl.ds((k % 16) * LANES, LANES)] = wide[:, k, :].astype(BF16)

    def block(part, b_index, a_index):
        return (b_index, a_index) if part == 0 else (a_index, b_index)

    first = ("x", "y")
    second = ("y", "x")
    half_rows = QUARTER // 2
    gathers = []
    from_partner = []

    def share(part, index):
        ref = hid.at[2 * c + part, index[0], index[1]]
        from_partner.append(send(ref, ref, partner))

    for part in range(2):
        a, b = first[part], second[part]
        index = block(part, here[b], here[a])
        ref = hid.at[2 * c + part, index[0], index[1]]
        g = {"a": {}, "b": {}}
        g["a"]["from_down"] = send(ref, ref, to_up(a))
        g["a"]["from_up"] = send(ref, ref, to_down(a))
        gathers.append(g)

    def second_axis(part, rel, a_index):
        b = second[part]
        index = block(part, here[b], a_index)
        ref = hid.at[2 * c + part, index[0], index[1]]
        gathers[part]["b"][rel, "from_down"] = send(ref, ref, to_up(b))
        gathers[part]["b"][rel, "from_up"] = send(ref, ref, to_down(b))
        share(part, index)

    def halves(ref, k):
        return ref.at[:, pl.ds(k * half_rows, half_rows)]

    for part in range(2):
        second_axis(part, "own", here[first[part]])
    for part in range(2):
        a, b = first[part], second[part]
        q = 2 * c + part
        g = gathers[part]["a"]
        g["from_down"].wait_recv()
        index = block(part, here[b], down[a])
        ref = halves(hid.at[q, index[0], index[1]], 0)
        g["opp0"] = send(ref, ref, to_up(a))
        g["from_up"].wait_recv()
        index = block(part, here[b], up[a])
        ref = halves(hid.at[q, index[0], index[1]], 1)
        g["opp1"] = send(ref, ref, to_down(a))
    for part in range(2):
        a = first[part]
        second_axis(part, "down", down[a])
        second_axis(part, "up", up[a])
    for part in range(2):
        a = first[part]
        g = gathers[part]["a"]
        g["opp0"].wait_recv()
        g["opp1"].wait_recv()
        second_axis(part, "opp", opp[a])
    rels = {"own": here, "down": down, "up": up, "opp": opp}
    for rel in ("own", "down", "up", "opp"):
        for part in range(2):
            a, b = first[part], second[part]
            g = gathers[part]["b"]
            q = 2 * c + part
            for side, place, to in (("from_down", down, to_up), ("from_up", up, to_down)):
                g[rel, side].wait_recv()
                index = block(part, place[b], rels[rel][a])
                ref = hid.at[q, index[0], index[1]]
                if (rel in ("own", "up")) == (side == "from_down"):
                    g[rel, "opp"] = send(ref, ref, to(b))
                share(part, index)
    for rel in ("own", "down", "up", "opp"):
        for part in range(2):
            a, b = first[part], second[part]
            gathers[part]["b"][rel, "opp"].wait_recv()
            share(part, block(part, opp[b], rels[rel][a]))
    for copy in from_partner:
        copy.wait_recv()
    for copy in w_copies:
        copy.wait()

    logits[...] = jnp.zeros_like(logits)

    def logits_step(k, _):
        q, m = lax.div(k, 2), lax.rem(k, 2)
        rows = pl.ds(pl.multiple_of(m * 256, 256), 256)
        logits[rows, :] += lax.dot_general(
            wv[rows, pl.ds(pl.multiple_of(q * QUARTER, QUARTER), QUARTER)],
            hid[q].reshape(256, QUARTER),
            (((1,), (1,)), ((), ())),
            preferred_element_type=F32,
        )
        return 0

    lax.fori_loop(0, 8, logits_step, 0)

    lt = logits[...]
    vocab_dev = lt.shape[0]
    offset = ((zl * 4 + x) * 16 + zh * 8 + y * 2 + c) * vocab_dev
    columns = lax.broadcasted_iota(jnp.int32, (vocab_dev, 256), 0) + offset
    mask = columns == tgt_ref[...]
    local_max = jnp.max(lt, axis=0, keepdims=True)
    local_total = jnp.sum(jnp.exp(lt - local_max), axis=0, keepdims=True)
    local_target = jnp.sum(jnp.where(mask, lt, 0.0), axis=0, keepdims=True)

    def put(ref_rows, values):
        for k, v in enumerate(values):
            for j in range(2):
                ref_rows(2 * k + j, v[:, j * LANES : (j + 1) * LANES])

    def combined(ref):
        v = ref[...]
        mx = jnp.max(v[:, 0:2], axis=0)
        total = jnp.sum(v[:, 2:4] * jnp.exp(v[:, 0:2] - mx[None]), axis=0)
        target = jnp.sum(v[:, 4:6], axis=0)
        return mx, total, target

    stat[...] = jnp.zeros_like(stat)
    for k, v in enumerate((local_max, local_total, local_target)):
        for j in range(2):
            stat[0, pl.ds(2 * k + j, 1), :] = v[:, j * LANES : (j + 1) * LANES]
    arrivals = []
    for dz, dc in column:
        z_, c_ = in_column(dz, dc)
        arrivals.append(send(stat.at[0], st1.at[me], device(x, y, z_, c_)))
    st1[me] = stat[0]
    for copy in arrivals:
        copy.wait_recv()
    for k, v in enumerate(combined(st1)):
        stat[1, pl.ds(2 * k, 2), :] = v
    spot = y * 4 + x
    arrivals = []
    for dx, dy in plane:
        x_, y_ = in_plane(dx, dy)
        arrivals.append(send(stat.at[1], st2.at[spot], device(x_, y_, z, c)))
    st2[spot] = stat[1]
    for copy in arrivals:
        copy.wait_recv()
    mx, total, target = combined(st2)
    rows2 = lax.broadcasted_iota(jnp.int32, (2, LANES), 0) * LANES + lax.broadcasted_iota(jnp.int32, (2, LANES), 1)
    mine = spot * 16 + me
    loss_ref[0, 0] = jnp.sum(jnp.where(rows2 == mine, mx + jnp.log(total) - target, 0.0))
    inverse = 1.0 / total

    def flat(v):
        return jnp.concatenate([v[0:1], v[1:2]], axis=1)

    probs = jnp.exp(logits[...] - flat(mx)) * flat(inverse) - jnp.where(mask, 1.0, 0.0)
    pt[...] = probs.T.astype(BF16)

    tile = 512

    def product(q, n):
        start = pl.multiple_of(q * QUARTER + n * tile, tile)
        return jnp.dot(pt[...], wv[:, pl.ds(start, tile)], preferred_element_type=F32).reshape(4, 4, 16, tile)

    swaps = []
    for part in range(2):
        q = 2 * (1 - c) + part

        def give_step(n, _, q=q, part=part):
            give[part, :, :, :, pl.ds(pl.multiple_of(n * tile, tile), tile)] = product(q, n).astype(BF16)
            return 0

        lax.fori_loop(0, QUARTER // tile, give_step, 0)
        swaps.append(send(give.at[part], take.at[part], partner))
    for part in range(2):
        q = 2 * c + part

        def own_step(n, _, q=q, part=part):
            own_sum[part, :, :, :, pl.ds(pl.multiple_of(n * tile, tile), tile)] = product(q, n)
            return 0

        lax.fori_loop(0, QUARTER // tile, own_step, 0)

    def chip_sum(part, index):
        return own_sum[part, index[0], index[1]] + take[part, index[0], index[1]].astype(F32)

    order = ("own", "up", "down", "opp")
    low, high = ("own", "up"), ("down", "opp")
    reds = [dict() for _ in range(2)]
    for part in range(2):
        a, b = first[part], second[part]
        swaps[part].wait_recv()
        r = reds[part]
        for rel in order:
            ub[part, 0, order.index(rel)] = chip_sum(part, block(part, opp[b], rels[rel][a])).astype(BF16)
            k = order.index(rel) % 2
            if rel in low:
                r["opp", rel] = send(ub.at[part, 0, order.index(rel)], vb_opp.at[part, order.index(rel)], to_up(b))
            else:
                r["opp", rel] = send(ub.at[part, 0, order.index(rel)], vb_opp.at[part, order.index(rel)], to_down(b))
    for part in range(2):
        a, b = first[part], second[part]
        r = reds[part]
        for rel in order:
            k = order.index(rel)
            if rel in high:
                slot, place, to = 0, up, to_up
            else:
                slot, place, to = 1, down, to_down
            ub[part, 1 + slot, k] = chip_sum(part, block(part, place[b], rels[rel][a])).astype(BF16)
            r[slot, rel] = send(ub.at[part, 1 + slot, k], vb_all.at[part, slot, k], to(b))
    for rel in order:
        for part in range(2):
            a, b = first[part], second[part]
            r = reds[part]
            k = order.index(rel)
            r["opp", rel].wait_recv()
            if rel in low:
                slot, place, to = 0, up, to_up
            else:
                slot, place, to = 1, down, to_down
            ub[part, 1 + slot, k] = (
                chip_sum(part, block(part, place[b], rels[rel][a])) + vb_opp[part, k].astype(F32)
            ).astype(BF16)
            r[slot, rel] = send(ub.at[part, 1 + slot, k], vb_all.at[part, slot, k], to(b))

    def line_sum(part, rel):
        a, b = first[part], second[part]
        k = order.index(rel)
        for slot in range(2):
            reds[part][slot, rel].wait_recv()
        return (
            chip_sum(part, block(part, here[b], rels[rel][a]))
            + vb_all[part, 0, k].astype(F32)
            + vb_all[part, 1, k].astype(F32)
        )

    half = QUARTER // 2
    for part in range(2):
        a = first[part]
        r = reds[part]
        ua[part, 0] = line_sum(part, "opp").astype(BF16)
        r["a_opp0"] = send(halves(ua.at[part, 0], 0), va_opp.at[part, 0], to_up(a))
        r["a_opp1"] = send(halves(ua.at[part, 0], 1), va_opp.at[part, 1], to_down(a))
    keep = {}
    for part in range(2):
        a = first[part]
        r = reds[part]
        for slot, rel, to in ((0, "up", to_up), (1, "down", to_down)):
            keep[part, slot] = line_sum(part, rel)
            own_half = 1 - slot
            ua[part, 1 + slot, :, pl.ds(own_half * half, half)] = keep[part, slot][
                :, own_half * half : (own_half + 1) * half
            ].astype(BF16)
            r["a", slot, own_half] = send(
                halves(ua.at[part, 1 + slot], own_half), va_all.at[part, slot, own_half], to(a)
            )
    for part in range(2):
        a = first[part]
        r = reds[part]
        for slot, to in ((0, to_up), (1, to_down)):
            r[f"a_opp{slot}"].wait_recv()
            ua[part, 1 + slot, :, pl.ds(slot * half, half)] = (
                keep[part, slot][:, slot * half : (slot + 1) * half] + va_opp[part, slot].astype(F32)
            ).astype(BF16)
            r["a", slot, slot] = send(halves(ua.at[part, 1 + slot], slot), va_all.at[part, slot, slot], to(a))
    for part in range(2):
        acc_a[part] = line_sum(part, "own")
    for part in range(2):
        r = reds[part]
        for k in range(2):
            for slot in range(2):
                r["a", slot, k].wait_recv()
            acc_a[part, :, pl.ds(k * half, half)] += va_all[part, 0, k].astype(F32) + va_all[part, 1, k].astype(F32)

    for k in range(32):
        rows_out[:, k, :] = acc_a[k // 16, :, pl.ds((k % 16) * LANES, LANES)]
    rows_b[...] = rows_out[...].astype(BF16)
    arrivals = []
    for dz, dc in column:
        z_, c_ = in_column(dz, dc)
        arrivals.append(send(rows_b.at[z_ * 2 + c_], rows_in.at[c, z], device(x, y, z_, c_)))
    rows_in[c, z] = jnp.zeros((32, LANES), BF16)
    for copy in arrivals:
        copy.wait_recv()
    summed = jnp.sum(rows_in[...].astype(F32), axis=1)
    row_f[...] = summed.reshape(64, LANES)
    row_f[pl.ds(pl.multiple_of(c * 32, 32), 32), :] += rows_out[me]
    grad_ref[...] = (row_f[...] * lg_ref[0, 0]).astype(BF16)

    for copy in pending:
        copy.wait_send()


COPIES = 512


def shards(hidden, weight, targets, loss_grad):
    order = targets.reshape(4, 4, 2, 4, 2).transpose(3, 1, 2, 0, 4).reshape(1, 256)
    vmem = pltpu.VMEM
    loss, grad = pl.pallas_call(
        kernel,
        out_shape=(jax.ShapeDtypeStruct((1, 1), F32), jax.ShapeDtypeStruct((64, LANES), BF16)),
        in_specs=[
            pl.BlockSpec(memory_space=pltpu.VMEM),
            pl.BlockSpec(memory_space=pl.ANY),
            pl.BlockSpec(memory_space=pltpu.VMEM),
            pl.BlockSpec(memory_space=pltpu.SMEM),
        ],
        out_specs=(pl.BlockSpec(memory_space=pltpu.SMEM), pl.BlockSpec(memory_space=pltpu.VMEM)),
        scratch_shapes=[
            vmem(weight.shape, BF16),
            vmem((64, LANES), F32),
            vmem((64, LANES), BF16),
            vmem((16, 32, LANES), BF16),
            vmem((16, 32, LANES), F32),
            vmem((4, 4, 4, 16, QUARTER), BF16),
            vmem((512, 256), F32),
            vmem((256, 512), BF16),
            vmem((2, 8, LANES), F32),
            vmem((16, 8, LANES), F32),
            vmem((16, 8, LANES), F32),
            vmem((2, 4, 4, 16, QUARTER), F32),
            vmem((2, 4, 4, 16, QUARTER), BF16),
            vmem((2, 4, 4, 16, QUARTER), BF16),
            vmem((2, 3, 4, 16, QUARTER), BF16),
            vmem((2, 4, 16, QUARTER), BF16),
            vmem((2, 2, 4, 16, QUARTER), BF16),
            vmem((2, 3, 16, QUARTER), BF16),
            vmem((2, 2, 16, QUARTER // 2), BF16),
            vmem((2, 2, 2, 16, QUARTER // 2), BF16),
            vmem((2, 16, QUARTER), F32),
            vmem((16, 32, LANES), F32),
            vmem((16, 32, LANES), BF16),
            vmem((2, 8, 32, LANES), BF16),
            pltpu.SemaphoreType.DMA((4,)),
            pltpu.SemaphoreType.DMA((COPIES,)),
            pltpu.SemaphoreType.DMA((COPIES,)),
        ],
        compiler_params=pltpu.CompilerParams(
            collective_id=0, has_side_effects=True, vmem_limit_bytes=60 * 1024 * 1024
        ),
    )(hidden, weight, order, loss_grad.reshape(1, 1))
    return loss.reshape(1), grad.reshape(1, 8192)


def solution(mesh):
    finer = Mesh(mesh.devices.reshape(4, 4, 2, 4, 2), AXES)
    whole = ("zl", "x", "zh", "y", "c")
    return jax.shard_map(
        shards,
        mesh=finer,
        in_specs=(P(whole, None), P(whole, None), P(), P(whole)),
        out_specs=(P(whole), P(whole, None)),
        check_vma=False,
    )
```

time: 329 us -> 92.3 us (0.28)
  waiting for transfers between devices: 183 us -> 0 us
  blocking collectives: 93.1 us -> 0 us
  Pallas kernels: 0 us -> 86 us
  matrix products: 16.2 us -> 0 us
  starting transfers between devices: 16.1 us -> 0 us
  between operations: 14.8 us -> 3.07 us
    reduce_scatter x1 -> x0, waiting for transfers between devices: 97.7 us -> none  [shards(): lax.psum_scatter(jnp.dot(probs_grad, weight, preferred_element_type=jnp.f...]
    all_gather x6 -> x0, blocking collectives: 93.1 us -> none  [the longest x5 56.7 us: collected_together(): both, at, found = (lax.all_gather(jnp.concatenate(lines), axis), 0, {})]
    pallas_call x0 -> x1, Pallas kernels: none -> 86 us  [shards(): pl.pallas_call(kernel, out_shape=(jax.ShapeDtypeStruct((1, 1), F32), jax....]
    all_gather x1 -> x0, waiting for transfers between devices: 72.8 us -> none  [shards(): lax.all_gather(section_block, SECTION, axis=0, tiled=True)]
    dot_general x2 -> x0, matrix products: 16.2 us -> none  [the longest x1 9.08 us: shards(): jnp.dot(probs_grad, weight, preferred_element_type=jnp.float32)]
    all_to_all x1 -> x0, starting transfers between devices: 16 us -> none  [sent_and_summed(): lax.all_to_all(cut_along(array, dim, peers), axis, 0, 0, tiled=True)]
    all_to_all x1 -> x0, waiting for transfers between devices: 12.3 us -> none  [sent_and_summed(): lax.all_to_all(cut_along(array, dim, peers), axis, 0, 0, tiled=True)]
  transfers between devices with their start and end apart: 3 -> 0, of which waited for: 3 -> 0; matrix products, arithmetic and copies ran while one was open for 0% -> 0% of each run, Pallas kernels for 0% -> 0%
where the time goes in v1:
time: 92.3 us; the launch traced here: 92 us
  Pallas kernels  86 us (93%)
  between operations  3.07 us (3%)
  local copies, waits for them, and re-layouts  2.95 us (3%)
    pallas_call x1, Pallas kernels, shards(): pl.pallas_call(kernel, out_shape=(jax.ShapeDtypeStruct((1, 1), F32), jax....  86 us

profile of v1, /device:TPU:1, one launch (start us, length us, event | category | flops | bytes accessed | tf_op | source)
XLA Modules:
  0.0 92.0 jit_solution(17242491833666072803)
XLA Ops:
  0.6 0.8 reshape.19
  1.5 0.7 reshape.20.tgt_ref
  2.9 86.0 %shard_map.59 = (f32[1,1]{1,0:T(1,128)}, bf16[64,128]{1,0:T(8,128)(2,1)}) custom-call(bf16[1,8192]{1,0:T(2,128)(2,1)} %h_ref.1, bf16[512,8192]{1,0:T(8,128)(2,1)} %w_hbm.1, s32[1,256]{1,0:T(1,128)} %reshape.20.tgt_ref, f32[1,1]{1,0:T(1,128)} %bitcast.8.lg_ref), custom_call_target="tpu_custom_call" | custom-call | tf_op jit(solution)/shard_map/pallas_call | solution.py:398
  88.9 1.4 %copy.9 = bf16[1,1,64,128]{3,1,2,0:T(2,128)(2,1)} copy(bf16[1,1,64,128]{3,2,1,0:T(8,128)(2,1)} %bitcast.11) | data formatting | bytes 32768
  (1 shorter events, 0.0 us)

commit v2 on v0

v2 whole, which is shorter than its diff:
```python
import jax
import jax.numpy as jnp
from jax import lax
from jax.experimental import pallas as pl
from jax.experimental.pallas import tpu as pltpu
from jax.sharding import Mesh
from jax.sharding import PartitionSpec as P

AXES = ("zl", "x", "zh", "y", "c")
F32, BF16 = jnp.float32, jnp.bfloat16
SLAB = 2048
PART = 1024
HALF = 512
LANES = 128
SENDS, RECVS = 24, 132
MESH = pl.DeviceIdType.MESH


def kernel(
    h_ref, w_hbm, tgt_ref, lg_ref, loss_ref, grad_ref,
    wv, wp, row_f, row_b, got, wide, hid, logits, logits_p, pt, stz, stz1, stz2, stt, stt1, stt2,
    own_sum, ub, vb_opp, vb_all, keep, ua, va_opp, va_all, acc, rows_out, rows_b, rows_in,
    w_sem, send_sem, recv_sem,
):
    zl, x, zh, y, c = (lax.axis_index(a) for a in AXES)
    z = zh * 4 + zl
    me, spot = z * 2 + c, y * 4 + x
    counts = {"send": 0, "recv": 0}
    ends = []

    def new(kind, sem):
        counts[kind] += 1
        return sem.at[counts[kind] - 1]

    def new_recv():
        return new("recv", recv_sem)

    def new_send(ref):
        s = new("send", send_sem)
        ends.append((s, ref))
        return s

    def take(sem, ref):
        pltpu.make_async_copy(ref, ref, sem).wait()

    def send(src, dst, to, s, r):
        pltpu.make_async_remote_copy(
            src_ref=src, dst_ref=dst, send_sem=s, recv_sem=r, device_id=to, device_id_type=MESH
        ).start()

    def device(x_, y_, z_, c_):
        return (lax.rem(z_, 4), x_, lax.div(z_, 4), y_, c_)

    up = {"x": lax.rem(x + 1, 4), "y": lax.rem(y + 1, 4)}
    opp = {"x": lax.rem(x + 2, 4), "y": lax.rem(y + 2, 4)}
    down = {"x": lax.rem(x + 3, 4), "y": lax.rem(y + 3, 4)}
    here = {"x": x, "y": y}
    rels = {"own": here, "down": down, "up": up, "opp": opp}
    first, second = ("x", "y"), ("y", "x")
    order = ("own", "up", "down", "opp")

    def to_up(axis):
        return device(up["x"] if axis == "x" else x, up["y"] if axis == "y" else y, z, c)

    def to_down(axis):
        return device(down["x"] if axis == "x" else x, down["y"] if axis == "y" else y, z, c)

    partner = device(x, y, z, 1 - c)
    column = [(dz, dc) for dz in (4, 3, 5, 2, 6, 1, 7, 0) for dc in range(2) if (dz, dc) != (0, 0)]
    plane = [(dx, dy) for dx in (2, 1, 3, 0) for dy in (2, 1, 3, 0) if (dx, dy) != (0, 0)]

    def in_column(dz, dc):
        return lax.rem(z + dz, 8), lax.rem(c + dc, 2)

    def in_plane(dx, dy):
        return lax.rem(x + dx, 4), lax.rem(y + dy, 4)

    def block(part, b_index, a_index):
        return (b_index, a_index) if part == 0 else (a_index, b_index)

    halfway = SLAB * 2
    w_copies = []
    for k, half in enumerate((1 - c, c)):
        cols = pl.ds(pl.multiple_of(half * halfway, halfway), halfway)
        w_copies.append(pltpu.make_async_copy(w_hbm.at[:, cols], wv.at[:, cols], w_sem.at[k]))
        w_copies[-1].start()

    barrier = pltpu.get_barrier_semaphore()
    for dz, dc in column:
        z_, c_ = in_column(dz, dc)
        pl.semaphore_signal(barrier, inc=1, device_id=device(x, y, z_, c_), device_id_type=MESH)
    for dx, dy in plane:
        x_, y_ = in_plane(dx, dy)
        pl.semaphore_signal(barrier, inc=1, device_id=device(x_, y_, z, c), device_id_type=MESH)

    for k in range(64):
        row_f[pl.ds(k, 1), :] = h_ref[:, pl.ds(k * LANES, LANES)].astype(F32)
    row_b[...] = row_f[...].astype(BF16)

    chip_base = ((zl * 4 + x) * 16 + zh * 8 + y * 2) * 512
    rel = tgt_ref[...] - chip_base
    near = jnp.logical_and(rel >= 0, rel < 1024)
    high = jnp.where(near, lax.shift_right_logical(rel, 4), 128)
    low = jnp.where(near, jnp.bitwise_and(rel, 15), 0)
    digit = lax.broadcasted_iota(jnp.int32, (16, 256), 0)
    digits = jnp.where(digit == 0, high, jnp.where(digit == 1, low, 0)).astype(F32).astype(BF16)
    r = lax.broadcasted_iota(jnp.int32, (256, 256), 1)
    t = lax.broadcasted_iota(jnp.int32, (256, 256), 0)
    bits = jnp.bitwise_and
    shift = lax.shift_right_logical
    token = (
        bits(shift(r, 1), 3) * 64 + bits(shift(r, 4), 3) * 16 + bits(shift(r, 3), 1) * 8 + shift(r, 6) * 2 + bits(r, 1)
    )
    moves = jnp.where(t == token, 1.0, 0.0).astype(BF16)
    placed = jnp.dot(digits, moves, preferred_element_type=F32)
    chip_row = (placed[0:1] * 16.0 + placed[1:2]).astype(jnp.int32)

    pl.semaphore_wait(barrier, len(column) + len(plane))

    col_recv = []
    for s in range(2):
        ss, rr = new_send(got.at[s, pl.ds(0, 15)]), new_recv()
        for dz, dc in column:
            z_, c_ = in_column(dz, dc)
            rows = pl.ds(pl.multiple_of(c_ * 32 + s * 16, 16), 16)
            send(row_b.at[rows], got.at[s, me], device(x, y, z_, c_), ss, rr)
        got[s, me] = row_b[pl.ds(pl.multiple_of(c * 32 + s * 16, 16), 16), :]
        col_recv.append(rr)

    a_send = new_send(hid.at[pl.ds(0, 3), 0, pl.ds(0, 2)])
    b_send = new_send(hid.at[pl.ds(0, 3), pl.ds(0, 2)])
    share_send = new_send(hid.at[pl.ds(0, 2)])
    share_recv = [new_recv() for _ in range(2)]
    w_send, w_recv = new_send(wp), new_recv()
    a_recv = {(s, p, k): new_recv() for s in range(2) for p in range(2) for k in ("down", "up", "opp")}
    b_recv = {
        (s, p, side, k): new_recv()
        for s in range(2) for p in range(2) for side in ("down", "up") for k in ("own", "next", "opp", "far")
    }

    def blk(s, p, index, cols=None):
        lo, n = (p * PART, PART) if cols is None else (p * PART + cols * HALF, HALF)
        return hid.at[2 * c + s, index[0], index[1], :, pl.ds(lo, n)]

    def share(s, p, index):
        ref = blk(s, p, index)
        send(ref, ref, partner, share_send, share_recv[s])

    def w_piece(k):
        src = wv.at[pl.ds(64 * k, 64), pl.ds(pl.multiple_of((1 - c) * halfway, halfway), halfway)]
        send(src, wp.at[pl.ds(64 * k, 64)], partner, w_send, w_recv)

    def second_axis(s, p, name, group):
        b = second[p]
        index = block(p, here[b], rels[name][first[p]])
        ref = blk(s, p, index)
        send(ref, ref, to_up(b), b_send, b_recv[s, p, "down", group])
        send(ref, ref, to_down(b), b_send, b_recv[s, p, "up", group])
        share(s, p, index)

    def step_c(s):
        take(col_recv[s], got.at[s, pl.ds(0, 15)])
        wide[...] = got[s].astype(F32)
        for k in range(16):
            hid[2 * c + s, y, x, :, pl.ds(k * LANES, LANES)] = wide[:, k, :].astype(BF16)
        for p in range(2):
            a = first[p]
            ref = blk(s, p, (y, x))
            send(ref, ref, to_up(a), a_send, a_recv[s, p, "down"])
            send(ref, ref, to_down(a), a_send, a_recv[s, p, "up"])
        for p in range(2):
            second_axis(s, p, "own", "own")

    def step_a1(s):
        for p in range(2):
            a, b = first[p], second[p]
            for k, (name, to) in enumerate((("down", to_up), ("up", to_down))):
                index = block(p, here[b], rels[name][a])
                take(a_recv[s, p, name], blk(s, p, index))
                ref = blk(s, p, index, k)
                send(ref, ref, to(a), a_send, a_recv[s, p, "opp"])
        for p in range(2):
            for name in ("down", "up"):
                second_axis(s, p, name, "next")

    def step_a2(s):
        for p in range(2):
            take(a_recv[s, p, "opp"], blk(s, p, block(p, here[second[p]], opp[first[p]])))
            second_axis(s, p, "opp", "opp")

    def step_b(s, group):
        names = {"own": ("own",), "next": ("down", "up"), "opp": ("opp",)}[group]
        for p in range(2):
            a, b = first[p], second[p]
            for side, place, to in (("down", down, to_up), ("up", up, to_down)):
                refs = [(n, block(p, place[b], rels[n][a])) for n in names]
                some = hid.at[2 * c + s, 0, pl.ds(0, len(names)), :, pl.ds(0, PART)]
                take(b_recv[s, p, side, group], some)
                for n, index in refs:
                    if (n in ("own", "up")) == (side == "down"):
                        ref = blk(s, p, index)
                        send(ref, ref, to(b), b_send, b_recv[s, p, side, "far"])
                for n, index in refs:
                    share(s, p, index)

    def step_far(s):
        for p in range(2):
            a, b = first[p], second[p]
            for side, names in (("down", ("own", "up")), ("up", ("down", "opp"))):
                take(b_recv[s, p, side, "far"], hid.at[2 * c + s, 0, pl.ds(0, 2), :, pl.ds(0, PART)])
                for n in names:
                    share(s, p, block(p, opp[b], rels[n][a]))

    def step_logits(s, half, start=False):
        v = half * 2 + s
        part = lax.dot_general(
            wv[:, pl.ds(pl.multiple_of(v * SLAB, SLAB), SLAB)],
            hid[v].reshape(256, SLAB),
            (((1,), (1,)), ((), ())),
            preferred_element_type=F32,
        )
        if start:
            logits[...] = part
        else:
            logits[...] += part

    w_copies[0].wait()
    step_c(0)
    step_a1(0)
    step_c(1)
    w_piece(0)
    step_a2(0)
    step_b(0, "own")
    w_piece(1)
    step_a1(1)
    w_piece(2)
    step_b(0, "next")
    w_piece(3)
    step_a2(1)
    step_b(0, "opp")
    w_piece(4)
    step_b(1, "own")
    w_piece(5)
    w_copies[1].wait()
    step_far(0)
    w_piece(6)
    step_b(1, "next")
    w_piece(7)
    step_logits(0, c, True)
    step_b(1, "opp")
    take(share_recv[0], hid.at[0])
    step_logits(0, 1 - c)
    step_far(1)
    step_logits(1, c)
    take(share_recv[1], hid.at[0])
    step_logits(1, 1 - c)

    swap_send, swap_recv = new_send(logits), new_recv()
    send(logits, logits_p, partner, swap_send, swap_recv)
    lt = logits[...]
    vocab_row = lax.broadcasted_iota(jnp.int32, (512, 256), 0)
    mask = vocab_row + c * 512 == chip_row
    local_max = jnp.max(lt, axis=0, keepdims=True)
    local_total = jnp.sum(jnp.exp(lt - local_max), axis=0, keepdims=True)

    def put(ref, row, v):
        for j in range(2):
            ref[0, pl.ds(row + j, 1), :] = v[:, j * LANES : (j + 1) * LANES]

    def over_column(src, dst):
        ss, rr = new_send(dst.at[pl.ds(0, 15)]), new_recv()
        for dz, dc in column:
            z_, c_ = in_column(dz, dc)
            send(src.at[0], dst.at[me], device(x, y, z_, c_), ss, rr)
        dst[me] = src[0]
        return rr

    def over_plane(src, dst):
        ss, rr = new_send(dst.at[pl.ds(0, 15)]), new_recv()
        for dx, dy in plane:
            x_, y_ = in_plane(dx, dy)
            send(src.at[1], dst.at[spot], device(x_, y_, z, c), ss, rr)
        dst[spot] = src[1]
        return rr

    def combined(ref):
        v = ref[...]
        mx = jnp.max(v[:, 0:2], axis=0)
        total = jnp.sum(v[:, 2:4] * jnp.exp(v[:, 0:2] - mx[None]), axis=0)
        return mx, total

    put(stz, 0, local_max)
    put(stz, 2, local_total)
    rr = over_column(stz, stz1)
    put(stt, 0, jnp.sum(jnp.where(mask, lt, 0.0), axis=0, keepdims=True))
    tt = over_column(stt, stt1)
    take(rr, stz1.at[pl.ds(0, 15)])
    for k, v in enumerate(combined(stz1)):
        stz[1, pl.ds(2 * k, 2), :] = v
    rr = over_plane(stz, stz2)
    take(tt, stt1.at[pl.ds(0, 15)])
    stt[1] = jnp.sum(stt1[...], axis=0)
    tt = over_plane(stt, stt2)
    take(swap_recv, logits_p)
    take(w_recv, wp)
    take(rr, stz2.at[pl.ds(0, 15)])
    mx, total = combined(stz2)

    def flat(v):
        return jnp.concatenate([v[0:1], v[1:2]], axis=1)

    mx_row, inverse = flat(mx), flat(1.0 / total)
    for k, (ref, half) in enumerate(((logits, c), (logits_p, 1 - c))):
        here_mask = vocab_row + half * 512 == chip_row
        probs = jnp.exp(ref[...] - mx_row) * inverse - jnp.where(here_mask, 1.0, 0.0)
        pt[k] = probs.T.astype(BF16)

    low_names, high_names = ("own", "up"), ("down", "opp")
    ub_send, ua_send = new_send(ub), new_send(ua)
    rb = {
        (s, p, k): new_recv() for s in range(2) for p in range(2)
        for k in ("opp0", "opp1", (0, "plain"), (0, "sum"), (1, "plain"), (1, "sum"))
    }
    ra = {
        (s, p, k): new_recv() for s in range(2) for p in range(2)
        for k in ("opp0", "opp1", (0, "plain"), (0, "sum"), (1, "plain"), (1, "sum"))
    }

    def product(s, p):
        def tile(n, _):
            at = s * SLAB + p * PART + n * HALF
            mine = pl.ds(pl.multiple_of(c * halfway + at, HALF), HALF)
            theirs = pl.ds(pl.multiple_of(at, HALF), HALF)
            out = jnp.dot(pt[0], wv[:, mine], preferred_element_type=F32) + jnp.dot(
                pt[1], wp[:, theirs], preferred_element_type=F32
            )
            own_sum[s, p, :, :, :, pl.ds(pl.multiple_of(n * HALF, HALF), HALF)] = out.reshape(4, 4, 16, HALF)
            return 0

        lax.fori_loop(0, PART // HALF, tile, 0)

    def mine_of(s, p, index):
        return own_sum[s, p, index[0], index[1]]

    def red_far(s, p):
        a, b = first[p], second[p]
        for n in order:
            k = order.index(n)
            ub[s, p, 0, k] = mine_of(s, p, block(p, opp[b], rels[n][a])).astype(BF16)
            if n in low_names:
                send(ub.at[s, p, 0, k], vb_opp.at[s, p, k], to_up(b), ub_send, rb[s, p, "opp0"])
            else:
                send(ub.at[s, p, 0, k], vb_opp.at[s, p, k], to_down(b), ub_send, rb[s, p, "opp1"])

    def red_plain(s, p):
        a, b = first[p], second[p]
        for n in order:
            k = order.index(n)
            slot, place, to = (0, up, to_up) if n in high_names else (1, down, to_down)
            ub[s, p, 1 + slot, k] = mine_of(s, p, block(p, place[b], rels[n][a])).astype(BF16)
            send(ub.at[s, p, 1 + slot, k], vb_all.at[s, p, slot, k], to(b), ub_send, rb[s, p, (slot, "plain")])

    def red_sum(s, p):
        a, b = first[p], second[p]
        take(rb[s, p, "opp0"], vb_opp.at[s, p, pl.ds(0, 2)])
        take(rb[s, p, "opp1"], vb_opp.at[s, p, pl.ds(2, 2)])
        for n in order:
            k = order.index(n)
            slot, place, to = (0, up, to_up) if n in low_names else (1, down, to_down)
            value = mine_of(s, p, block(p, place[b], rels[n][a])) + vb_opp[s, p, k].astype(F32)
            ub[s, p, 1 + slot, k] = value.astype(BF16)
            send(ub.at[s, p, 1 + slot, k], vb_all.at[s, p, slot, k], to(b), ub_send, rb[s, p, (slot, "sum")])

    def line_sum(s, p, name):
        k = order.index(name)
        index = block(p, here[second[p]], rels[name][first[p]])
        return mine_of(s, p, index) + vb_all[s, p, 0, k].astype(F32) + vb_all[s, p, 1, k].astype(F32)

    def half_of(ref, k):
        return ref.at[:, pl.ds(k * HALF, HALF)]

    def red_line(s, p):
        a = first[p]
        for slot in range(2):
            for kind in ("plain", "sum"):
                take(rb[s, p, (slot, kind)], vb_all.at[s, p, slot, pl.ds(0, 2)])
        ua[s, p, 0] = line_sum(s, p, "opp").astype(BF16)
        send(half_of(ua.at[s, p, 0], 0), va_opp.at[s, p, 0], to_up(a), ua_send, ra[s, p, "opp0"])
        send(half_of(ua.at[s, p, 0], 1), va_opp.at[s, p, 1], to_down(a), ua_send, ra[s, p, "opp1"])
        for slot, name, to in ((0, "up", to_up), (1, "down", to_down)):
            value = line_sum(s, p, name)
            keep[s, p, slot] = value
            k = 1 - slot
            ua[s, p, 1 + slot, :, pl.ds(k * HALF, HALF)] = value[:, k * HALF : (k + 1) * HALF].astype(BF16)
            send(half_of(ua.at[s, p, 1 + slot], k), va_all.at[s, p, slot, k], to(a), ua_send, ra[s, p, (slot, "plain")])
        acc[s, p] = line_sum(s, p, "own")

    def red_line_sum(s, p):
        a = first[p]
        for slot, to in ((0, to_up), (1, to_down)):
            take(ra[s, p, f"opp{slot}"], va_opp.at[s, p, slot])
            value = keep[s, p, slot, :, pl.ds(slot * HALF, HALF)] + va_opp[s, p, slot].astype(F32)
            ua[s, p, 1 + slot, :, pl.ds(slot * HALF, HALF)] = value.astype(BF16)
            send(half_of(ua.at[s, p, 1 + slot], slot), va_all.at[s, p, slot, slot], to(a), ua_send, ra[s, p, (slot, "sum")])

    def red_end(s, p):
        for slot in range(2):
            for kind in ("plain", "sum"):
                take(ra[s, p, (slot, kind)], va_all.at[s, p, slot, 0])
        for k in range(2):
            acc[s, p, :, pl.ds(k * HALF, HALF)] += va_all[s, p, 0, k].astype(F32) + va_all[s, p, 1, k].astype(F32)

    def both(step, s):
        for p in range(2):
            step(s, p)

    row_recv = []

    def rows_step(s):
        for k in range(16):
            rows_out[s, :, k, :] = acc[s, k // 8, :, pl.ds((k % 8) * LANES, LANES)]
        rows_b[s] = rows_out[s].astype(BF16)
        ss, rr = new_send(rows_b.at[s, pl.ds(0, 15)]), new_recv()
        for dz, dc in column:
            z_, c_ = in_column(dz, dc)
            send(rows_b.at[s, z_ * 2 + c_], rows_in.at[s, c, z], device(x, y, z_, c_), ss, rr)
        rows_in[s, c, z] = jnp.zeros((16, LANES), BF16)
        row_recv.append(rr)

    for p in range(2):
        product(0, p)
        red_far(0, p)
        red_plain(0, p)
    for p in range(2):
        product(1, p)
        red_far(1, p)
    both(red_sum, 0)
    both(red_plain, 1)
    both(red_sum, 1)
    both(red_line, 0)
    both(red_line_sum, 0)
    both(red_end, 0)
    rows_step(0)
    both(red_line, 1)
    both(red_line_sum, 1)
    both(red_end, 1)
    rows_step(1)

    take(tt, stt2.at[pl.ds(0, 15)])
    target = jnp.sum(stt2[...], axis=0)
    place2 = lax.broadcasted_iota(jnp.int32, (2, LANES), 0) * LANES + lax.broadcasted_iota(jnp.int32, (2, LANES), 1)
    loss_ref[0, 0] = jnp.sum(jnp.where(place2 == spot * 16 + me, mx + jnp.log(total) - target, 0.0))

    for s in range(2):
        take(row_recv[s], rows_b.at[s, pl.ds(0, 15)])
        summed = jnp.sum(rows_in[s].astype(F32), axis=1)
        for half in range(2):
            row_f[pl.ds(half * 32 + s * 16, 16), :] = summed[half]
        row_f[pl.ds(pl.multiple_of(c * 32 + s * 16, 16), 16), :] += rows_out[s, me]
    row_f[...] = row_f[...] * lg_ref[0]
    for k in range(64):
        grad_ref[:, pl.ds(k * LANES, LANES)] = row_f[pl.ds(k, 1), :].astype(BF16)

    for sem, ref in ends:
        take(sem, ref)
    assert counts["send"] <= SENDS and counts["recv"] <= RECVS, counts


def shards(hidden, weight, targets, loss_grad):
    vmem = pltpu.VMEM
    loss, grad = pl.pallas_call(
        kernel,
        out_shape=(jax.ShapeDtypeStruct((1, 1), F32), jax.ShapeDtypeStruct((1, 8192), BF16)),
        in_specs=[
            pl.BlockSpec(memory_space=pltpu.VMEM),
            pl.BlockSpec(memory_space=pl.ANY),
            pl.BlockSpec(memory_space=pltpu.VMEM),
            pl.BlockSpec(memory_space=pltpu.SMEM),
        ],
        out_specs=(pl.BlockSpec(memory_space=pltpu.SMEM), pl.BlockSpec(memory_space=pltpu.VMEM)),
        scratch_shapes=[
            vmem((512, 8192), BF16),
            vmem((512, 4096), BF16),
            vmem((64, LANES), F32),
            vmem((64, LANES), BF16),
            vmem((2, 16, 16, LANES), BF16),
            vmem((16, 16, LANES), F32),
            vmem((4, 4, 4, 16, SLAB), BF16),
            vmem((512, 256), F32),
            vmem((512, 256), F32),
            vmem((2, 256, 512), BF16),
            vmem((2, 4, LANES), F32),
            vmem((16, 4, LANES), F32),
            vmem((16, 4, LANES), F32),
            vmem((2, 2, LANES), F32),
            vmem((16, 2, LANES), F32),
            vmem((16, 2, LANES), F32),
            vmem((2, 2, 4, 4, 16, PART), F32),
            vmem((2, 2, 3, 4, 16, PART), BF16),
            vmem((2, 2, 4, 16, PART), BF16),
            vmem((2, 2, 2, 4, 16, PART), BF16),
            vmem((2, 2, 2, 16, PART), F32),
            vmem((2, 2, 3, 16, PART), BF16),
            vmem((2, 2, 2, 16, HALF), BF16),
            vmem((2, 2, 2, 2, 16, HALF), BF16),
            vmem((2, 2, 16, PART), F32),
            vmem((2, 16, 16, LANES), F32),
            vmem((2, 16, 16, LANES), BF16),
            vmem((2, 2, 8, 16, LANES), BF16),
            pltpu.SemaphoreType.DMA((2,)),
            pltpu.SemaphoreType.DMA((SENDS,)),
            pltpu.SemaphoreType.DMA((RECVS,)),
        ],
        compiler_params=pltpu.CompilerParams(
            collective_id=0, has_side_effects=True, vmem_limit_bytes=60 * 1024 * 1024
        ),
    )(hidden, weight, targets.reshape(1, 256), loss_grad)
    return loss.reshape(1), grad


def solution(mesh):
    finer = Mesh(mesh.devices.reshape(4, 4, 2, 4, 2), AXES)
    return jax.shard_map(
        shards,
        mesh=finer,
        in_specs=(P(AXES, None), P(AXES, None), P(), P(AXES)),
        out_specs=(P(AXES), P(AXES, None)),
        check_vma=False,
    )
```

time: 329 us -> 84.7 us (0.26)
  waiting for transfers between devices: 183 us -> 0 us
  blocking collectives: 93.1 us -> 0 us
  Pallas kernels: 0 us -> 80 us
  matrix products: 16.2 us -> 0 us
  starting transfers between devices: 16.1 us -> 0 us
  between operations: 14.8 us -> 3.04 us
    reduce_scatter x1 -> x0, waiting for transfers between devices: 97.7 us -> none  [shards(): lax.psum_scatter(jnp.dot(probs_grad, weight, preferred_element_type=jnp.f...]
    all_gather x6 -> x0, blocking collectives: 93.1 us -> none  [the longest x5 56.7 us: collected_together(): both, at, found = (lax.all_gather(jnp.concatenate(lines), axis), 0, {})]
    pallas_call x0 -> x1, Pallas kernels: none -> 80 us  [shards(): pl.pallas_call(kernel, out_shape=(jax.ShapeDtypeStruct((1, 1), F32), jax....]
    all_gather x1 -> x0, waiting for transfers between devices: 72.8 us -> none  [shards(): lax.all_gather(section_block, SECTION, axis=0, tiled=True)]
    dot_general x2 -> x0, matrix products: 16.2 us -> none  [the longest x1 9.08 us: shards(): jnp.dot(probs_grad, weight, preferred_element_type=jnp.float32)]
    all_to_all x1 -> x0, starting transfers between devices: 16 us -> none  [sent_and_summed(): lax.all_to_all(cut_along(array, dim, peers), axis, 0, 0, tiled=True)]
    all_to_all x1 -> x0, waiting for transfers between devices: 12.3 us -> none  [sent_and_summed(): lax.all_to_all(cut_along(array, dim, peers), axis, 0, 0, tiled=True)]
  transfers between devices with their start and end apart: 3 -> 0, of which waited for: 3 -> 0; matrix products, arithmetic and copies ran while one was open for 0% -> 0% of each run, Pallas kernels for 0% -> 0%
where the time goes in v2:
time: 84.7 us; the launch traced here: 84.5 us
  Pallas kernels  80 us (94%)
  between operations  3.04 us (4%)
  local copies, waits for them, and re-layouts  1.41 us (2%)
    pallas_call x1, Pallas kernels, shards(): pl.pallas_call(kernel, out_shape=(jax.ShapeDtypeStruct((1, 1), F32), jax....  80 us

profile of v2, /device:TPU:1, one launch (start us, length us, event | category | flops | bytes accessed | tf_op | source)
XLA Modules:
  0.0 84.5 jit_solution(8741028979206213002)
XLA Ops:
  1.3 80.0 %shard_map.59 = (f32[1,1]{1,0:T(1,128)}, bf16[1,8192]{1,0:T(2,128)(2,1)}) custom-call(bf16[1,8192]{1,0:T(2,128)(2,1)} %h_ref.1, bf16[512,8192]{1,0:T(8,128)(2,1)} %w_hbm.1, s32[1,256]{1,0:T(1,128)} %bitcast.2, f32[1]{0:T(128)S(6)} %copy.8.lg_ref), custom_call_target="tpu_custom_call" | custom-call | tf_op jit(solution)/shard_map/pallas_call | solution.py:471
  81.9 1.4 %copy.10 = bf16[1,8192]{1,0:T(2,128)(2,1)} copy(bf16[1,8192]{1,0:T(2,128)(2,1)} %get-tuple-element.9) | data formatting | bytes 32768

commit v3 on v2

v3 whole, which is shorter than its diff:
```python
import jax
import jax.numpy as jnp
from jax import lax
from jax.experimental import pallas as pl
from jax.experimental.pallas import tpu as pltpu
from jax.sharding import Mesh
from jax.sharding import PartitionSpec as P

AXES = ("zl", "x", "zh", "y", "c")
F32, BF16 = jnp.float32, jnp.bfloat16
PART = 2048
LANES = 128
TURN = 1024
SENDS, RECVS = 16, 68
MESH = pl.DeviceIdType.MESH


def kernel(
    h_hbm, w_hbm, tgt_hbm, lg_ref, loss_ref, grad_ref,
    h_ref, tgt_ref, wt, part_logits,
    wv, wp, row_f, row_b, got, wide, hid, logits, logits_p, pt, stz, stz1, stz2,
    own_sum, ub, vb_opp, vb_all, ua, va, acc, rows_out, rows_b, rows_in,
    w_sem, send_sem, recv_sem,
):
    zl, x, zh, y, c = (lax.axis_index(a) for a in AXES)
    z = zh * 4 + zl
    me, spot = z * 2 + c, y * 4 + x
    counts = {"send": 0, "recv": 0}
    ends = []

    def new(kind, sem):
        counts[kind] += 1
        return sem.at[counts[kind] - 1]

    def new_recv():
        return new("recv", recv_sem)

    def new_send(ref):
        s = new("send", send_sem)
        ends.append((s, ref))
        return s

    def take(sem, ref):
        pltpu.make_async_copy(ref, ref, sem).wait()

    def send(src, dst, to, s, r):
        pltpu.make_async_remote_copy(
            src_ref=src, dst_ref=dst, send_sem=s, recv_sem=r, device_id=to, device_id_type=MESH
        ).start()

    def device(x_, y_, z_, c_):
        return (lax.rem(z_, 4), x_, lax.div(z_, 4), y_, c_)

    up = {"x": lax.rem(x + 1, 4), "y": lax.rem(y + 1, 4)}
    opp = {"x": lax.rem(x + 2, 4), "y": lax.rem(y + 2, 4)}
    down = {"x": lax.rem(x + 3, 4), "y": lax.rem(y + 3, 4)}
    here = {"x": x, "y": y}
    rels = {"own": here, "down": down, "up": up, "opp": opp}
    first, second = ("x", "y"), ("y", "x")
    order = ("own", "up", "down", "opp")

    def to_up(axis):
        return device(up["x"] if axis == "x" else x, up["y"] if axis == "y" else y, z, c)

    def to_opp(axis):
        return device(opp["x"] if axis == "x" else x, opp["y"] if axis == "y" else y, z, c)

    def to_down(axis):
        return device(down["x"] if axis == "x" else x, down["y"] if axis == "y" else y, z, c)

    partner = device(x, y, z, 1 - c)
    column = [(dz, dc) for dz in (4, 3, 5, 2, 6, 1, 7, 0) for dc in range(2) if (dz, dc) != (0, 0)]
    plane = [(dx, dy) for dx in (2, 1, 3, 0) for dy in (2, 1, 3, 0) if (dx, dy) != (0, 0)]

    def in_column(dz, dc):
        return lax.rem(z + dz, 8), lax.rem(c + dc, 2)

    def in_plane(dx, dy):
        return lax.rem(x + dx, 4), lax.rem(y + dy, 4)

    def block(part, b_index, a_index):
        return (b_index, a_index) if part == 0 else (a_index, b_index)

    barrier = pltpu.get_barrier_semaphore()
    for dz, dc in column:
        z_, c_ = in_column(dz, dc)
        pl.semaphore_signal(barrier, inc=1, device_id=device(x, y, z_, c_), device_id_type=MESH)
    for dx, dy in plane:
        x_, y_ = in_plane(dx, dy)
        pl.semaphore_signal(barrier, inc=1, device_id=device(x_, y_, z, c), device_id_type=MESH)

    small = [pltpu.make_async_copy(h_hbm, h_ref, w_sem.at[2]), pltpu.make_async_copy(tgt_hbm, tgt_ref, w_sem.at[3])]
    for copy in small:
        copy.start()
    halfway = PART * 2
    w_copies = []
    for k, half in enumerate((1 - c, c)):
        cols = pl.ds(pl.multiple_of(half * halfway, halfway), halfway)
        w_copies.append(pltpu.make_async_copy(w_hbm.at[:, cols], wv.at[:, cols], w_sem.at[k]))
        w_copies[-1].start()

    for copy in small:
        copy.wait()

    for k in range(64):
        row_f[pl.ds(k, 1), :] = h_ref[:, pl.ds(k * LANES, LANES)].astype(F32)
    row_b[...] = row_f[...].astype(BF16)

    chip_base = ((zl * 4 + x) * 16 + zh * 8 + y * 2) * 512
    rel = tgt_ref[...] - chip_base
    near = jnp.logical_and(rel >= 0, rel < 1024)
    high = jnp.where(near, lax.shift_right_logical(rel, 4), 128)
    low = jnp.where(near, jnp.bitwise_and(rel, 15), 0)
    digit = lax.broadcasted_iota(jnp.int32, (16, 256), 0)
    digits = jnp.where(digit == 0, high, jnp.where(digit == 1, low, 0)).astype(F32).astype(BF16)
    r = lax.broadcasted_iota(jnp.int32, (256, 256), 1)
    t = lax.broadcasted_iota(jnp.int32, (256, 256), 0)
    bits = jnp.bitwise_and
    shift = lax.shift_right_logical
    token = (
        bits(shift(r, 1), 3) * 64 + bits(shift(r, 3), 3) * 16 + shift(r, 7) * 8 + bits(shift(r, 5), 3) * 2 + bits(r, 1)
    )
    moves = jnp.where(t == token, 1.0, 0.0).astype(BF16)
    placed = jnp.dot(digits, moves, preferred_element_type=F32)
    chip_row = (placed[0:1] * 16.0 + placed[1:2]).astype(jnp.int32)

    pl.semaphore_wait(barrier, len(column) + len(plane))

    ss, both_recv = new_send(got.at[pl.ds(0, 15)]), [new_recv(), new_recv()]
    base = counts["recv"] - 2
    for dz, dc in column:
        z_, c_ = in_column(dz, dc)
        rows = pl.ds(pl.multiple_of(c_ * 32, 32), 32)
        send(row_b.at[rows], got.at[me], device(x, y, z_, c_), ss, recv_sem.at[base + zh])
    rows = pl.ds(pl.multiple_of(c * 32, 32), 32)
    pltpu.make_async_copy(row_b.at[rows], got.at[me], recv_sem.at[base + zh]).start()

    a_send = new_send(hid.at[0, 0, pl.ds(0, 3), pl.ds(0, 2)])
    not_own = ("down", "up", "opp")
    b_send = new_send(hid.at[0, pl.ds(0, 2), pl.ds(0, 3)])
    share_send = new_send(hid.at[0])
    share_recv = [new_recv() for _ in range(2)]
    w_send, w_recv = new_send(wp), new_recv()
    a_recv = {(s, p): new_recv() for s in range(2) for p in range(2)}
    b_recv = {
        (s, p, side, k): new_recv()
        for s in range(2) for p in range(2) for side in ("down", "up") for k in ("own", "rest", "far")
    }

    def blk(s, p, index):
        return hid.at[s, c, index[0], index[1], :, pl.ds(p * PART, PART)]

    def share(s, p, index):
        ref = blk(s, p, index)
        send(ref, ref, partner, share_send, share_recv[s])

    def w_piece(k):
        src = wv.at[pl.ds(64 * k, 64), pl.ds(pl.multiple_of((1 - c) * halfway, halfway), halfway)]
        send(src, wp.at[pl.ds(64 * k, 64)], partner, w_send, w_recv)

    def second_axis(s, p, name, group):
        b = second[p]
        index = block(p, here[b], rels[name][first[p]])
        ref = blk(s, p, index)
        send(ref, ref, to_up(b), b_send, b_recv[s, p, "down", group])
        send(ref, ref, to_down(b), b_send, b_recv[s, p, "up", group])
        share(s, p, index)

    def step_c(s):
        take(both_recv[s], got.at[pl.ds(0, 8)])
        wide[...] = got[pl.ds(8 * s, 8)].astype(F32)
        for k in range(32):
            hid[s, c, y, x, :, pl.ds(k * LANES, LANES)] = wide[:, k, :].astype(BF16)
        for p in range(2):
            a = first[p]
            ref = blk(s, p, (y, x))
            for to in (to_up, to_down, to_opp):
                send(ref, ref, to(a), a_send, a_recv[s, p])
        for p in range(2):
            second_axis(s, p, "own", "own")

    def step_a(s):
        for p in range(2):
            take(a_recv[s, p], hid.at[s, 0, 0, pl.ds(0, 3), :, pl.ds(0, PART)])
            for name in not_own:
                second_axis(s, p, name, "rest")

    def step_b(s, group):
        names = {"own": ("own",), "rest": not_own}[group]
        for p in range(2):
            a, b = first[p], second[p]
            for side, place, to in (("down", down, to_up), ("up", up, to_down)):
                refs = [(n, block(p, place[b], rels[n][a])) for n in names]
                some = hid.at[s, 0, 0, pl.ds(0, len(names)), :, pl.ds(0, PART)]
                take(b_recv[s, p, side, group], some)
                for n, index in refs:
                    if (n in ("own", "up")) == (side == "down"):
                        ref = blk(s, p, index)
                        send(ref, ref, to(b), b_send, b_recv[s, p, side, "far"])
                for n, index in refs:
                    share(s, p, index)

    def step_far(s):
        for p in range(2):
            a, b = first[p], second[p]
            for side, names in (("down", ("own", "up")), ("up", ("down", "opp"))):
                take(b_recv[s, p, side, "far"], hid.at[s, 0, 0, pl.ds(0, 2), :, pl.ds(0, PART)])
                for n in names:
                    share(s, p, block(p, opp[b], rels[n][a]))

    def turn(n):
        def piece(k, _):
            at = pl.ds(pl.multiple_of(n * TURN + k * 256, 256), 256)
            wt[at, :] = wv[:, at].T
            return 0

        lax.fori_loop(0, TURN // 256, piece, 0)

    def step_logits(s, half, start=False):
        part = jnp.dot(
            hid[s, half].reshape(128, halfway),
            wt[pl.ds(pl.multiple_of(half * halfway, halfway), halfway), :],
            preferred_element_type=F32,
        )
        if start:
            part_logits[...] = part
        else:
            logits[s] = (part_logits[...] + part).T

    vocab_row = lax.broadcasted_iota(jnp.int32, (512, 128), 0)
    chunk_row = [chip_row[:, s * 128 : (s + 1) * 128] for s in range(2)]
    swap_send = new_send(logits)
    swap_recv = [new_recv() for _ in range(2)]
    stat_recv = {}

    def stat_local(s):
        send(logits.at[s], logits_p.at[s], partner, swap_send, swap_recv[s])
        lt = logits[s]
        mask = vocab_row + c * 512 == chunk_row[s]
        local_max = jnp.max(lt, axis=0, keepdims=True)
        stz[s, 0, pl.ds(0, 1), :] = local_max
        stz[s, 0, pl.ds(1, 1), :] = jnp.sum(jnp.exp(lt - local_max), axis=0, keepdims=True)
        stz[s, 0, pl.ds(2, 1), :] = jnp.sum(jnp.where(mask, lt, 0.0), axis=0, keepdims=True)
        ss, stat_recv[s, 0] = new_send(stz1.at[s, pl.ds(0, 15)]), new_recv()
        for dz, dc in column:
            z_, c_ = in_column(dz, dc)
            send(stz.at[s, 0], stz1.at[s, me], device(x, y, z_, c_), ss, stat_recv[s, 0])
        stz1[s, me] = stz[s, 0]

    def combined(v):
        mx = jnp.max(v[:, 0:1], axis=0)
        total = jnp.sum(v[:, 1:2] * jnp.exp(v[:, 0:1] - mx[None]), axis=0)
        return mx, total, jnp.sum(v[:, 2:3], axis=0)

    def stat_column(s):
        take(stat_recv[s, 0], stz1.at[s, pl.ds(0, 15)])
        for k, v in enumerate(combined(stz1[s])):
            stz[s, 1, pl.ds(k, 1), :] = v
        ss, stat_recv[s, 1] = new_send(stz2.at[s, pl.ds(0, 15)]), new_recv()
        for dx, dy in plane:
            x_, y_ = in_plane(dx, dy)
            send(stz.at[s, 1], stz2.at[s, spot], device(x_, y_, z, c), ss, stat_recv[s, 1])
        stz2[s, spot] = stz[s, 1]

    def probs(s):
        take(stat_recv[s, 1], stz2.at[s, pl.ds(0, 15)])
        take(swap_recv[s], logits_p.at[s])
        mx, total, target = combined(stz2[s])
        column_id = lax.broadcasted_iota(jnp.int32, (1, LANES), 1)
        chosen = jnp.logical_and(column_id == spot * 8 + zl * 2 + c, zh == s)
        loss = jnp.sum(jnp.where(chosen, mx + jnp.log(total) - target, 0.0))
        inverse = 1.0 / total
        for k, (ref, half) in enumerate(((logits, c), (logits_p, 1 - c))):
            mask = vocab_row + half * 512 == chunk_row[s]
            value = jnp.exp(ref[s] - mx) * inverse - jnp.where(mask, 1.0, 0.0)
            pt[s, k] = value.T.astype(BF16)
        return loss

    low_names, high_names = ("own", "up"), ("down", "opp")
    ub_send, ua_send = new_send(ub), new_send(ua)
    rb = {
        (s, p, k): new_recv() for s in range(2) for p in range(2)
        for k in ("opp0", "opp1", (0, "plain"), (0, "sum"), (1, "plain"), (1, "sum"))
    }
    ra = {(s, p): new_recv() for s in range(2) for p in range(2)}

    def product(s, p):
        mine = pl.ds(pl.multiple_of(c * halfway + p * PART, PART), PART)
        theirs = pl.ds(p * PART, PART)
        out = jnp.dot(pt[s, 0], wv[:, mine], preferred_element_type=F32) + jnp.dot(
            pt[s, 1], wp[:, theirs], preferred_element_type=F32
        )
        own_sum[s, p] = out.reshape(4, 4, 8, PART)

    def mine_of(s, p, index):
        return own_sum[s, p, index[0], index[1]]

    def red_far(s, p):
        a, b = first[p], second[p]
        for n in order:
            k = order.index(n)
            ub[s, p, 0, k] = mine_of(s, p, block(p, opp[b], rels[n][a])).astype(BF16)
            if n in low_names:
                send(ub.at[s, p, 0, k], vb_opp.at[s, p, k], to_up(b), ub_send, rb[s, p, "opp0"])
            else:
                send(ub.at[s, p, 0, k], vb_opp.at[s, p, k], to_down(b), ub_send, rb[s, p, "opp1"])

    def red_plain(s, p):
        a, b = first[p], second[p]
        for n in order:
            k = order.index(n)
            slot, place, to = (0, up, to_up) if n in high_names else (1, down, to_down)
            ub[s, p, 1 + slot, k] = mine_of(s, p, block(p, place[b], rels[n][a])).astype(BF16)
            send(ub.at[s, p, 1 + slot, k], vb_all.at[s, p, slot, k], to(b), ub_send, rb[s, p, (slot, "plain")])

    def red_sum(s, p):
        a, b = first[p], second[p]
        take(rb[s, p, "opp0"], vb_opp.at[s, p, pl.ds(0, 2)])
        take(rb[s, p, "opp1"], vb_opp.at[s, p, pl.ds(2, 2)])
        for n in order:
            k = order.index(n)
            slot, place, to = (0, up, to_up) if n in low_names else (1, down, to_down)
            value = mine_of(s, p, block(p, place[b], rels[n][a])) + vb_opp[s, p, k].astype(F32)
            ub[s, p, 1 + slot, k] = value.astype(BF16)
            send(ub.at[s, p, 1 + slot, k], vb_all.at[s, p, slot, k], to(b), ub_send, rb[s, p, (slot, "sum")])

    def line_sum(s, p, name):
        k = order.index(name)
        index = block(p, here[second[p]], rels[name][first[p]])
        return mine_of(s, p, index) + vb_all[s, p, 0, k].astype(F32) + vb_all[s, p, 1, k].astype(F32)

    def red_line(s, p):
        a = first[p]
        for slot in range(2):
            for kind in ("plain", "sum"):
                take(rb[s, p, (slot, kind)], vb_all.at[s, p, slot, pl.ds(0, 2)])
        for k, (name, to) in enumerate((("opp", to_opp), ("up", to_up), ("down", to_down))):
            ua[s, p, k] = line_sum(s, p, name).astype(BF16)
            send(ua.at[s, p, k], va.at[s, p, k], to(a), ua_send, ra[s, p])
        acc[s, p] = line_sum(s, p, "own")

    def red_end(s, p):
        take(ra[s, p], va.at[s, p])
        acc[s, p] += jnp.sum(va[s, p].astype(F32), axis=0)

    def both(step, s):
        for p in range(2):
            step(s, p)

    row_recv, row_send, last_send = new_recv(), [], []

    def rows_step(s):
        for k in range(32):
            rows_out[:, k, :] = acc[s, k // 16, :, pl.ds((k % 16) * LANES, LANES)]
        rows_b[s] = rows_out[...].astype(BF16)
        ss = new_send(rows_b.at[s, pl.ds(0, 7)])
        counts["send"] += 1
        straight = send_sem.at[counts["send"] - 1]
        for dz in (2, 1, 3, 0):
            for dc in (1, 0):
                zl_, c_ = lax.rem(zl + dz, 4), lax.rem(c + dc, 2)
                src, dst = rows_b.at[s, zl_ * 2 + c_], rows_in.at[c, z]
                to = device(x, y, zl_ + 4 * s, c_)
                if dz or dc:
                    send(src, dst, to, ss, row_recv)
                else:

                    @pl.when(zh == s)
                    def _(src=src, dst=dst):
                        pltpu.make_async_copy(src, dst, row_recv).start()

                    @pl.when(zh != s)
                    def _(src=src, dst=dst, to=to):
                        send(src, dst, to, straight, row_recv)

        last_send.append((s, straight))

    w_copies[0].wait()
    for n in range(4):
        turn((1 - c) * 4 + n)
    w_copies[1].wait()
    for n in range(4):
        turn(c * 4 + n)
    step_c(0)
    step_c(1)
    w_piece(0)
    w_piece(1)
    step_a(0)
    step_b(0, "own")
    w_piece(2)
    step_a(1)
    w_piece(3)
    step_b(0, "rest")
    w_piece(4)
    step_b(1, "own")
    w_piece(5)
    step_far(0)
    w_piece(6)
    step_logits(0, c, True)
    step_b(1, "rest")
    w_piece(7)
    take(share_recv[0], hid.at[0, 0])
    step_logits(0, 1 - c)
    stat_local(0)
    step_far(1)
    step_logits(1, c, True)
    take(share_recv[1], hid.at[0, 0])
    step_logits(1, 1 - c)
    stat_local(1)
    stat_column(0)
    take(w_recv, wp)
    loss = probs(0)
    for p in range(2):
        product(0, p)
        red_far(0, p)
        red_plain(0, p)
    stat_column(1)
    both(red_sum, 0)
    loss += probs(1)
    loss_ref[0, 0] = loss
    for p in range(2):
        product(1, p)
        red_far(1, p)
    both(red_plain, 1)
    both(red_line, 0)
    both(red_sum, 1)
    both(red_end, 0)
    rows_step(0)
    both(red_line, 1)
    both(red_end, 1)
    rows_step(1)

    take(row_recv, rows_in)
    row_f[...] = jnp.sum(rows_in[...].astype(F32), axis=1).reshape(64, LANES) * lg_ref[0]
    for k in range(64):
        grad_ref[:, pl.ds(k * LANES, LANES)] = row_f[pl.ds(k, 1), :].astype(BF16)

    for s, sem in last_send:

        @pl.when(zh != s)
        def _(s=s, sem=sem):
            take(sem, rows_b.at[s, 0])

    for sem, ref in ends:
        take(sem, ref)
    assert counts == {"send": SENDS, "recv": RECVS}, counts


def shards(hidden, weight, targets, loss_grad):
    vmem = pltpu.VMEM
    loss, grad = pl.pallas_call(
        kernel,
        out_shape=(jax.ShapeDtypeStruct((1, 1), F32), jax.ShapeDtypeStruct((1, 8192), BF16)),
        in_specs=[
            pl.BlockSpec(memory_space=pl.ANY),
            pl.BlockSpec(memory_space=pl.ANY),
            pl.BlockSpec(memory_space=pl.ANY),
            pl.BlockSpec(memory_space=pltpu.SMEM),
        ],
        out_specs=(pl.BlockSpec(memory_space=pltpu.SMEM), pl.BlockSpec(memory_space=pltpu.VMEM)),
        scratch_shapes=[
            vmem((1, 8192), BF16),
            vmem((1, 256), jnp.int32),
            vmem((8192, 512), BF16),
            vmem((128, 512), F32),
            vmem((512, 8192), BF16),
            vmem((512, 4096), BF16),
            vmem((64, LANES), F32),
            vmem((64, LANES), BF16),
            vmem((16, 32, LANES), BF16),
            vmem((8, 32, LANES), F32),
            vmem((2, 2, 4, 4, 8, 2 * PART), BF16),
            vmem((2, 512, LANES), F32),
            vmem((2, 512, LANES), F32),
            vmem((2, 2, 128, 512), BF16),
            vmem((2, 2, 3, LANES), F32),
            vmem((2, 16, 3, LANES), F32),
            vmem((2, 16, 3, LANES), F32),
            vmem((2, 2, 4, 4, 8, PART), F32),
            vmem((2, 2, 3, 4, 8, PART), BF16),
            vmem((2, 2, 4, 8, PART), BF16),
            vmem((2, 2, 2, 4, 8, PART), BF16),
            vmem((2, 2, 3, 8, PART), BF16),
            vmem((2, 2, 3, 8, PART), BF16),
            vmem((2, 2, 8, PART), F32),
            vmem((8, 32, LANES), F32),
            vmem((2, 8, 32, LANES), BF16),
            vmem((2, 8, 32, LANES), BF16),
            pltpu.SemaphoreType.DMA((4,)),
            pltpu.SemaphoreType.DMA((SENDS,)),
            pltpu.SemaphoreType.DMA((RECVS,)),
        ],
        compiler_params=pltpu.CompilerParams(
            collective_id=0, has_side_effects=True, vmem_limit_bytes=60 * 1024 * 1024
        ),
    )(hidden, weight, targets.reshape(1, 256), loss_grad)
    return loss.reshape(1), grad


def solution(mesh):
    finer = Mesh(mesh.devices.reshape(4, 4, 2, 4, 2), AXES)
    return jax.shard_map(
        shards,
        mesh=finer,
        in_specs=(P(AXES, None), P(AXES, None), P(), P(AXES)),
        out_specs=(P(AXES), P(AXES, None)),
        check_vma=False,
    )
```

time: 84.7 us -> 68.9 us (0.81); the launches traced: 84.5 us -> 67.7 us
  Pallas kernels: 80 us -> 63.2 us
    pallas_call x1, Pallas kernels: 80 us -> 63.2 us  [shards(): pl.pallas_call(kernel, out_shape=(jax.ShapeDtypeStruct((1, 1), F32), jax....]
where the time goes in v3:
time: 68.9 us; the launch traced here: 67.7 us
  Pallas kernels  63.2 us (92%)
  between operations  3.04 us (4%)
  local copies, waits for them, and re-layouts  1.41 us (2%)
    pallas_call x1, Pallas kernels, shards(): pl.pallas_call(kernel, out_shape=(jax.ShapeDtypeStruct((1, 1), F32), jax....  63.2 us
    unnamed x1, local copies, waits for them, and re-layouts  1.41 us

profile of v3, /device:TPU:1, one launch (start us, length us, event | category | flops | bytes accessed | tf_op | source)
XLA Modules:
  0.0 67.7 jit_solution(7777383285428508867)
XLA Ops:
  1.3 63.2 %shard_map.59 = (f32[1,1]{1,0:T(1,128)}, bf16[1,8192]{1,0:T(2,128)(2,1)}) custom-call(bf16[1,8192]{1,0:T(2,128)(2,1)} %h_hbm.1, bf16[512,8192]{1,0:T(8,128)(2,1)} %w_hbm.1, s32[1,256]{1,0:T(1,128)} %bitcast.2, f32[1]{0:T(128)S(6)} %copy.8.lg_ref), custom_call_target="tpu_custom_call" | custom-call | tf_op jit(solution)/shard_map/pallas_call | solution.py:451
  65.1 1.4 %copy.10 = bf16[1,8192]{1,0:T(2,128)(2,1)} copy(bf16[1,8192]{1,0:T(2,128)(2,1)} %get-tuple-element.9) | data formatting | bytes 32768
